TPU v7x, 32 devices: a whole 2x2x4 slice. The times are simulated.
32 devices in a mesh: row: 4 (over x, core), col: 8 (over z, y).
Axes of the slice: x: 2, y: 2, z: 4, core: 2. Of those that a mesh axis runs over, the one named last changes fastest.
Arguments:
- ancestor_inverse: bfloat16 [24576, 24576], P('row', 'col'), may hold values from -0.0390625 to 0.0390625
- panels: bfloat16 [24576, 3, 512], P(('row', 'col')), may hold values from -1.1953125 to 1.1953125
- diag_inverse: float32 [3, 512, 512], replicated, may hold values from -6 to 6
- tile_mask: int32 [3, 192], replicated, may hold values 0 or 1
Outputs:
- off_diagonal: float32 [24576, 3, 512], P(('row', 'col'))
- diagonal: float32 [3, 512, 512], replicated
All inputs are finite; a program needn't handle non-finite values.
Results may differ from a plain program's by a relative error of at most 0.0003.
Values may be sent and summed in bfloat16 or wider, within the bound.
A program may use at most 192 MiB of HBM per device.

v0:
```python
import jax
import jax.numpy as jnp
from jax import lax
from jax.sharding import PartitionSpec as P


def exchange(partial, axis):
    count = lax.axis_size(axis)
    rows, width = partial.shape
    return lax.psum_scatter(partial, axis, scatter_dimension=0, tiled=True)


def body(ancestor_inverse, panels, diag_inverse, tile_mask):
    row_count = lax.axis_size("row")
    col_count = lax.axis_size("col")
    span = lax.axis_index("row") * col_count + lax.axis_index("col")
    kept_rows = panels.shape[0]
    panel_count = panels.shape[1]
    tile = kept_rows * row_count * col_count // tile_mask.shape[1]
    full_mask = jnp.repeat(tile_mask, tile, axis=1).astype(jnp.bfloat16)
    own_mask = lax.dynamic_slice_in_dim(full_mask, span * kept_rows, kept_rows, 1)
    moves = [
        (index, index % row_count * col_count + index // row_count)
        for index in range(row_count * col_count)
    ]
    masked = [panels[:, p, :] * own_mask[p][:, None] for p in range(panel_count)]
    sent = [lax.ppermute(block, ("row", "col"), moves) for block in masked]
    sides = [lax.all_gather(block, "row", axis=0, tiled=True) for block in sent]
    results, parts = ([], [])
    for p in range(panel_count):
        partial = jnp.dot(ancestor_inverse, sides[p], preferred_element_type=jnp.float32)
        summed = -exchange(partial, "col")
        results.append(summed)
        parts.append(
            lax.dot_general(
                masked[p].astype(jnp.float32),
                summed,
                (((0,), (0,)), ((), ())),
                precision=lax.Precision.HIGHEST,
            )
        )
    off_diagonal = jnp.stack(results, axis=1)
    schur = lax.psum(jnp.stack(parts), ("row", "col"))
    return (off_diagonal, diag_inverse - schur)


def solution(mesh):
    return jax.shard_map(
        body,
        mesh=mesh,
        in_specs=(P("row", "col"), P(("row", "col"), None, None), P(), P()),
        out_specs=(P(("row", "col"), None, None), P()),
        check_vma=False,
    )
```

profile of v0, /device:TPU:0, one launch (start us, length us, event | category | flops | bytes accessed | tf_op | source)
XLA Modules:
  0.0 952.1 jit_solution(13903537531053839367)
XLA Ops:
  7.2 0.7 convert_element_type.10
  8.3 2.0 bitcast_multiply_fusion.2
  10.3 1.6 collective-permute-start.2
  12.0 1.6 collective-permute-start
  13.6 1.5 collective-permute-start.1
  15.2 86.4 %all-gather.8.cloned.1.call-done = bf16[3072,512]{1,0:T(8,128)(2,1)} async-done(((bf16[768,512]{1,0:T(8,128)(2,1)}), bf16[3072,512]{1,0:T(8,128)(2,1)}) %all-gather.8.cloned.1.call-update) | async-done | bytes 3145744 | tf_op jit(solution)/shard_map/all_gather | solution.py:28
  101.6 27.8 %convolution_bitcast_fusion = f32[6144,512]{0,1:T(8,128)} fusion(bf16[3072,512]{1,0:T(8,128)(2,1)} %all-gather.8.cloned.1.call-done, bf16[6144,3072]{1,0:T(8,128)(2,1)} %param.4), kind=kOutput, calls=%fused_computation | convolution fusion | flops 19327352832 | bytes 53477376 | tf_op jit(solution)/shard_map/dot_general | solution.py:31
  129.7 5.6 all-gather.4.cloned.1.call-done
  135.3 27.7 %convolution_bitcast_fusion.2 = f32[6144,512]{0,1:T(8,128)} fusion(bf16[3072,512]{1,0:T(8,128)(2,1)} %all-gather.4.cloned.1.call-done, bf16[6144,3072]{1,0:T(8,128)(2,1)} %param.4), kind=kOutput, calls=%fused_computation.2 | convolution fusion | flops 19327352832 | bytes 53477376 | tf_op jit(solution)/shard_map/dot_general | solution.py:31
  163.3 3.3 all-gather.6.cloned.1.call-done
  166.6 27.7 %convolution_bitcast_fusion.1 = f32[6144,512]{0,1:T(8,128)} fusion(bf16[3072,512]{1,0:T(8,128)(2,1)} %all-gather.6.cloned.1.call-done, bf16[6144,3072]{1,0:T(8,128)(2,1)} %param.4), kind=kOutput, calls=%fused_computation.1 | convolution fusion | flops 19327352832 | bytes 53477376 | tf_op jit(solution)/shard_map/dot_general | solution.py:31
  194.6 182.9 %reduce-scatter.8.cloned.1.call-done = f32[768,512]{0,1:T(8,128)} async-done(((f32[6144,512]{0,1:T(8,128)}), f32[768,512]{0,1:T(8,128)}) %reduce-scatter.8.cloned.1.call-update) | async-done | bytes 1572880 | tf_op jit(solution)/shard_map/reduce_scatter | solution.py:10
  377.5 3.1 fusion.12
  380.7 206.9 %reduce-scatter.4.cloned.1.call-done = f32[768,512]{0,1:T(8,128)} async-done(((f32[6144,512]{0,1:T(8,128)}), f32[768,512]{0,1:T(8,128)}) %reduce-scatter.4.cloned.1.call-update) | async-done | bytes 1572880 | tf_op jit(solution)/shard_map/reduce_scatter | solution.py:10
  587.6 3.4 fusion.6
  590.9 206.7 %reduce-scatter.6.cloned.1.call-done = f32[768,512]{0,1:T(8,128)} async-done(((f32[6144,512]{0,1:T(8,128)}), f32[768,512]{0,1:T(8,128)}) %reduce-scatter.6.cloned.1.call-update) | async-done | bytes 1572880 | tf_op jit(solution)/shard_map/reduce_scatter | solution.py:10
  797.6 3.1 fusion.9
  800.7 2.0 pad_maximum_fusion.1
  802.7 1.4 copy-done
  804.7 0.9 copy-done.1
  805.8 2.4 pad_maximum_fusion
  808.2 6.2 copy.6
  814.4 126.5 %all-reduce.2.cloned.1.call-done = f32[3,512,512]{2,1,0:T(8,128)} async-done(((f32[3,512,512]{2,1,0:T(8,128)}), f32[3,512,512]{2,1,0:T(8,128)}) %all-reduce.2.cloned.1.call-update) | async-done | bytes 3145744 | tf_op jit(solution)/shard_map/psum | solution.py:43
  941.0 4.3 sub.3
  (31 shorter events, 2.1 us)
Async XLA Ops:
  7.2 94.5 %all-gather.8.cloned.1.call-start = ((), (), s32[]{:S(2)}) async-start(), calls=%async_computation.7 | async-start | bytes 3932160 | tf_op jit(solution)/shard_map/all_gather | solution.py:28
  10.3 119.1 %copy-start.4 = (bf16[768,512]{1,0:T(8,128)(2,1)}, bf16[768,512]{1,0:T(8,128)(2,1)S(1)}, u32[]{:S(2)}) copy-start(bf16[768,512]{1,0:T(8,128)(2,1)S(1)} %get-tuple-element.7) | copy-start | bytes 2359300
  10.3 1.6 collective-permute-start.2
  11.9 123.4 %all-gather.4.cloned.1.call-start = ((), (), s32[]{:S(2)}) async-start(), calls=%async_computation.3 | async-start | bytes 3932160 | tf_op jit(solution)/shard_map/all_gather | solution.py:28
  12.0 1.6 collective-permute-start
  13.6 153.1 %all-gather.6.cloned.1.call-start = ((), (), s32[]{:S(2)}) async-start(), calls=%async_computation.5 | async-start | bytes 3932160 | tf_op jit(solution)/shard_map/all_gather | solution.py:28
  13.6 1.5 collective-permute-start.1
  15.2 362.4 %reduce-scatter.8.cloned.1.call-start = ((), (), s32[]{:S(2)}) async-start(), calls=%async_computation.8 | async-start | bytes 14155776 | tf_op jit(solution)/shard_map/reduce_scatter | solution.py:10
  129.4 458.1 %reduce-scatter.4.cloned.1.call-start = ((), (), s32[]{:S(2)}) async-start(), calls=%async_computation.4 | async-start | bytes 14155776 | tf_op jit(solution)/shard_map/reduce_scatter | solution.py:10
  163.1 634.6 %reduce-scatter.6.cloned.1.call-start = ((), (), s32[]{:S(2)}) async-start(), calls=%async_computation.6 | async-start | bytes 14155776 | tf_op jit(solution)/shard_map/reduce_scatter | solution.py:10
  194.3 746.7 %all-reduce.2.cloned.1.call-start = ((), (), s32[]{:S(2)}) async-start(), calls=%async_computation.9 | async-start | bytes 6291456 | tf_op jit(solution)/shard_map/psum | solution.py:43
  802.7 1.4 copy-start
  802.7 1.9 copy-start.2
  804.1 1.5 copy-start.1
  808.2 132.8 %copy-start.3 = (f32[3,512,512]{2,1,0:T(8,128)S(1)}, f32[3,512,512]{2,1,0:T(8,128)}, u32[]{:S(2)}) copy-start(f32[3,512,512]{2,1,0:T(8,128)} %param.6) | copy-start | bytes 9437188
Sparse Core Ops, SparseCore 0:
  12.0 89.5 all-gather.7
  103.2 32.0 all-gather.3
  136.9 29.7 all-gather.5
  170.0 207.4 reduce-scatter.7
  381.0 206.5 reduce-scatter.3
  591.0 206.5 reduce-scatter.5
  803.7 137.2 all-reduce.1
where the time goes:
time: 953 us; the launch traced here: 952 us
  waiting for transfers between devices  818 us (86%)
  matrix products  92.8 us (10%)
  between operations  14.2 us (1%)
  other arithmetic  11.7 us (1%)
    reduce_scatter x3, waiting for transfers between devices, exchange(): return lax.psum_scatter(partial, axis, scatter_dimension=0, tiled=True)  597 us
    psum x1, waiting for transfers between devices, body(): schur = lax.psum(jnp.stack(parts), ('row', 'col'))  127 us
    all_gather x3, waiting for transfers between devices, body(): sides = [lax.all_gather(block, 'row', axis=0, tiled=True) for block in sent]  95.3 us
    dot_general x3, matrix products, body(): jnp.dot(ancestor_inverse, sides[p], preferred_element_type=jnp.float32)  83.2 us
  transfers between devices with their start and end apart: 10, of which 7 were waited for; matrix products, arithmetic and copies ran while one was open for 10% of the time, Pallas kernels for 0%

commit v1 on v0

--- a/solution.py
+++ b/solution.py
@@ -40,7 +40,9 @@
             )
         )
     off_diagonal = jnp.stack(results, axis=1)
-    schur = lax.psum(jnp.stack(parts), ("row", "col"))
+    own = jnp.stack(parts)
+    blocks = lax.all_gather(own, ("row", "col"))
+    schur = jnp.sum(blocks, axis=0)
     return (off_diagonal, diag_inverse - schur)
 
 

time: 953 us -> 1360 us (1.43)
  waiting for transfers between devices: 818 us -> 1200 us
  other arithmetic: 11.7 us -> 42.5 us
    all_gather x0 -> x1, waiting for transfers between devices: none -> 504 us  [body(): blocks = lax.all_gather(own, ('row', 'col'))]
    psum x1 -> x0, waiting for transfers between devices: 127 us -> none  [body(): schur = lax.psum(jnp.stack(parts), ('row', 'col'))]
    reduce_sum x0 -> x1, other arithmetic: none -> 30.8 us  [body(): schur = jnp.sum(blocks, axis=0)]
  transfers between devices with their start and end apart: 10 -> 10, of which waited for: 7 -> 7; matrix products, arithmetic and copies ran while one was open for 10% -> 7% of each run, Pallas kernels for 0% -> 0%
where the time goes in v1:
time: 1360 us
  waiting for transfers between devices  1200 us (88%)
  matrix products  92.5 us (7%)
  other arithmetic  42.5 us (3%)
  between operations  14.2 us (1%)
    reduce_scatter x3, waiting for transfers between devices, exchange(): return lax.psum_scatter(partial, axis, scatter_dimension=0, tiled=True)  597 us
    all_gather x1, waiting for transfers between devices, body(): blocks = lax.all_gather(own, ('row', 'col'))  504 us
    all_gather x3, waiting for transfers between devices, body(): sides = [lax.all_gather(block, 'row', axis=0, tiled=True) for block in sent]  95.6 us
    dot_general x3, matrix products, body(): jnp.dot(ancestor_inverse, sides[p], preferred_element_type=jnp.float32)  82.9 us
    reduce_sum x1, other arithmetic, body(): schur = jnp.sum(blocks, axis=0)  30.8 us
  transfers between devices with their start and end apart: 10, of which 7 were waited for; matrix products, arithmetic and copies ran while one was open for 7% of the time, Pallas kernels for 0%

profile of v1, /device:TPU:0, one launch (start us, length us, event | category | flops | bytes accessed | tf_op | source)
XLA Modules:
  0.0 1360.4 jit_solution(12932539839666719789)
XLA Ops:
  8.3 2.0 bitcast_multiply_fusion.2
  10.3 1.6 collective-permute-start.1
  12.0 1.5 collective-permute-start.2
  13.6 1.5 collective-permute-start
  15.2 86.4 %all-gather.8.cloned.1.call-done = bf16[3072,512]{1,0:T(8,128)(2,1)} async-done(((bf16[768,512]{1,0:T(8,128)(2,1)}), bf16[3072,512]{1,0:T(8,128)(2,1)}) %all-gather.8.cloned.1.call-update) | async-done | bytes 3145744 | tf_op jit(solution)/shard_map/all_gather | solution.py:28
  101.6 27.7 %convolution_bitcast_fusion.1 = f32[6144,512]{0,1:T(8,128)} fusion(bf16[3072,512]{1,0:T(8,128)(2,1)} %all-gather.8.cloned.1.call-done, bf16[6144,3072]{1,0:T(8,128)(2,1)} %param.4), kind=kOutput, calls=%fused_computation.1 | convolution fusion | flops 19327352832 | bytes 53477376 | tf_op jit(solution)/shard_map/dot_general | solution.py:31
  129.6 5.7 all-gather.10.cloned.1.call-done
  135.3 27.6 %convolution_bitcast_fusion = f32[6144,512]{0,1:T(8,128)} fusion(bf16[3072,512]{1,0:T(8,128)(2,1)} %all-gather.10.cloned.1.call-done, bf16[6144,3072]{1,0:T(8,128)(2,1)} %param.4), kind=kOutput, calls=%fused_computation | convolution fusion | flops 19327352832 | bytes 53477376 | tf_op jit(solution)/shard_map/dot_general | solution.py:31
  163.2 3.4 all-gather.6.cloned.1.call-done
  166.6 27.6 %convolution_bitcast_fusion.2 = f32[6144,512]{0,1:T(8,128)} fusion(bf16[3072,512]{1,0:T(8,128)(2,1)} %all-gather.6.cloned.1.call-done, bf16[6144,3072]{1,0:T(8,128)(2,1)} %param.4), kind=kOutput, calls=%fused_computation.2 | convolution fusion | flops 19327352832 | bytes 53477376 | tf_op jit(solution)/shard_map/dot_general | solution.py:31
  194.6 183.0 %reduce-scatter.6.cloned.1.call-done = f32[768,512]{0,1:T(8,128)} async-done(((f32[6144,512]{0,1:T(8,128)}), f32[768,512]{0,1:T(8,128)}) %reduce-scatter.6.cloned.1.call-update) | async-done | bytes 1572880 | tf_op jit(solution)/shard_map/reduce_scatter | solution.py:10
  377.5 3.1 fusion.9
  380.7 206.9 %reduce-scatter.8.cloned.1.call-done = f32[768,512]{0,1:T(8,128)} async-done(((f32[6144,512]{0,1:T(8,128)}), f32[768,512]{0,1:T(8,128)}) %reduce-scatter.8.cloned.1.call-update) | async-done | bytes 1572880 | tf_op jit(solution)/shard_map/reduce_scatter | solution.py:10
  587.6 3.4 fusion.12
  590.9 206.7 %reduce-scatter.4.cloned.1.call-done = f32[768,512]{0,1:T(8,128)} async-done(((f32[6144,512]{0,1:T(8,128)}), f32[768,512]{0,1:T(8,128)}) %reduce-scatter.4.cloned.1.call-update) | async-done | bytes 1572880 | tf_op jit(solution)/shard_map/reduce_scatter | solution.py:10
  797.6 3.1 fusion.6
  800.7 2.0 pad_maximum_fusion.1
  802.7 1.4 copy-done
  804.7 0.9 copy-done.2
  805.8 2.4 pad_maximum_fusion
  808.2 6.5 copy.7
  814.7 503.8 %all-gather.12.cloned.1.call-done = f32[96,512,512]{2,1,0:T(8,128)} async-done(((f32[3,512,512]{2,1,0:T(8,128)}), f32[96,512,512]{2,1,0:T(8,128)}) %all-gather.12.cloned.1.call-update) | async-done | bytes 100663312 | tf_op jit(solution)/shard_map/all_gather | solution.py:44
  1318.5 30.8 %reduce_sum.9 = f32[3,512,512]{2,1,0:T(8,128)S(1)} reduce(f32[32,3,512,512]{3,2,1,0:T(8,128)} %bitcast.12, f32[]{:T(128)} %constant.17.clone.1), dimensions={0}, to_apply=%region_3.0 | reduce | flops 24379392 | bytes 103809024 | tf_op jit(solution)/shard_map/reduce_sum | solution.py:45
  1349.3 4.3 sub.3
  (30 shorter events, 2.8 us)
Async XLA Ops:
  7.2 94.5 %all-gather.8.cloned.1.call-start = ((), (), s32[]{:S(2)}) async-start(), calls=%async_computation.5 | async-start | bytes 3932160 | tf_op jit(solution)/shard_map/all_gather | solution.py:28
  10.3 119.0 %copy-start.3 = (bf16[768,512]{1,0:T(8,128)(2,1)}, bf16[768,512]{1,0:T(8,128)(2,1)S(1)}, u32[]{:S(2)}) copy-start(bf16[768,512]{1,0:T(8,128)(2,1)S(1)} %get-tuple-element.10) | copy-start | bytes 2359300
  10.3 1.6 collective-permute-start.1
  11.9 123.4 %all-gather.10.cloned.1.call-start = ((), (), s32[]{:S(2)}) async-start(), calls=%async_computation.7 | async-start | bytes 3932160 | tf_op jit(solution)/shard_map/all_gather | solution.py:28
  12.0 1.5 collective-permute-start.2
  13.5 153.1 %all-gather.6.cloned.1.call-start = ((), (), s32[]{:S(2)}) async-start(), calls=%async_computation.3 | async-start | bytes 3932160 | tf_op jit(solution)/shard_map/all_gather | solution.py:28
  13.6 1.5 collective-permute-start
  15.1 362.4 %reduce-scatter.6.cloned.1.call-start = ((), (), s32[]{:S(2)}) async-start(), calls=%async_computation.6 | async-start | bytes 14155776 | tf_op jit(solution)/shard_map/reduce_scatter | solution.py:10
  129.4 458.2 %reduce-scatter.8.cloned.1.call-start = ((), (), s32[]{:S(2)}) async-start(), calls=%async_computation.8 | async-start | bytes 14155776 | tf_op jit(solution)/shard_map/reduce_scatter | solution.py:10
  162.9 634.7 %reduce-scatter.4.cloned.1.call-start = ((), (), s32[]{:S(2)}) async-start(), calls=%async_computation.4 | async-start | bytes 14155776 | tf_op jit(solution)/shard_map/reduce_scatter | solution.py:10
  194.3 1124.2 %all-gather.12.cloned.1.call-start = ((), (), s32[]{:S(2)}) async-start(), calls=%async_computation.9 | async-start | bytes 103809024 | tf_op jit(solution)/shard_map/all_gather | solution.py:44
  802.7 1.4 copy-start
  802.7 1.9 copy-start.1
  804.1 1.5 copy-start.2
Sparse Core Ops, SparseCore 0:
  12.0 89.5 all-gather.7
  103.2 32.0 all-gather.9
  136.9 29.7 all-gather.5
  170.0 207.4 reduce-scatter.5
  381.0 206.5 reduce-scatter.7
  591.0 206.5 reduce-scatter.3
  802.9 515.5 all-gather.11
